TPU v7x, 32 devices: a whole 2x2x4 slice. The times are simulated.
32 devices in a mesh: dp: 4 (over y, core), tensor: 8 (over z, x).
Axes of the slice: x: 2, y: 2, z: 4, core: 2. Of those that a mesh axis runs over, the one named last changes fastest.
Arguments:
- grads: bfloat16 [4, 2, 7168, 2048], P('dp', None, 'tensor'), may hold values from -6 to 6
- master: float32 [2, 7168, 2048], P(None, 'dp', 'tensor'), may hold values from -0.0625 to 0.0625
- moment1: float32 [2, 7168, 2048], P(None, 'dp', 'tensor'), may hold values from -3 to 3
- moment2: float32 [2, 7168, 2048], P(None, 'dp', 'tensor'), may hold values from 1 to 30
- tokens: bfloat16 [1024, 7168], P('dp'), may hold values from -6 to 6
- route: int32 [512], P('dp'), may hold values from 0 to 255, as said below
Outputs:
- new_master: float32 [2, 7168, 2048], P(None, 'dp', 'tensor')
- new_moment1: float32 [2, 7168, 2048], P(None, 'dp', 'tensor')
- new_moment2: float32 [2, 7168, 2048], P(None, 'dp', 'tensor')
- rollout: bfloat16 [2, 7168, 2048], P(None, None, 'tensor')
- hidden: bfloat16 [512, 2048], P('dp', 'tensor')
Inputs may be any that keep to these rules, and one draw needn't show every extreme that they name: route[i] indexes one of the 256 tokens of the data rank that holds routed row i; within one data rank's 128 routed rows no token appears twice.
All inputs are finite; a program needn't handle non-finite values.
Results may differ from a plain program's by a relative error of at most 0.019.
Values may be sent and summed in bfloat16 or wider, within the bound.
A program may use at most 128 MiB of HBM per device.

v0:
```python
import jax
import jax.numpy as jnp
from jax import lax
from jax.sharding import PartitionSpec as P


def body(grads, master, moment1, moment2, tokens, route):
    tensor_count = lax.axis_size("tensor")
    rank_count = lax.axis_size("dp")
    grad_local = grads[0]
    rows_tensor = grad_local.shape[1]
    hidden_width = grad_local.shape[2]
    col_width = hidden_width // tensor_count
    slab = rows_tensor // rank_count
    summed = lax.psum_scatter(grad_local, "dp", scatter_dimension=1, tiled=True).astype(jnp.float32)
    pieces = summed.reshape(2, slab, tensor_count, col_width)
    spread = lax.all_to_all(
        pieces.astype(jnp.bfloat16), "tensor", split_axis=2, concat_axis=1, tiled=True
    ).astype(pieces.dtype)
    spread = spread.reshape(2, rank_count, tensor_count // rank_count, slab, col_width)
    owned = lax.all_to_all(
        spread.astype(jnp.bfloat16), "dp", split_axis=1, concat_axis=3, tiled=True
    ).astype(spread.dtype)
    grad_total = owned.reshape(2, rows_tensor * tensor_count // rank_count, col_width)
    new_moment1 = 0.9 * moment1 + 0.1 * grad_total
    new_moment2 = 0.95 * moment2 + 0.05 * grad_total * grad_total
    first_fix = 1.0 - 0.9**10
    second_fix = 1.0 - 0.95**10
    step_size = (
        new_moment1 / first_fix / (jnp.sqrt(new_moment2 / second_fix) + 1e-08) + 0.1 * master
    )
    new_master = master - 0.003 * step_size
    rollout_shard = new_master.astype(jnp.bfloat16)
    replicated = lax.all_gather(rollout_shard, "dp", axis=1, tiled=True)
    picked = jnp.take(tokens, route, axis=0)
    both = jnp.einsum("rd,kdh->rkh", picked, replicated, preferred_element_type=jnp.float32)
    hidden = (jax.nn.silu(both[:, 0, :]) * both[:, 1, :]).astype(jnp.bfloat16)
    return (new_master, new_moment1, new_moment2, replicated, hidden)


def solution(mesh):
    in_specs = (
        P("dp", None, "tensor", None),
        P(None, "dp", "tensor"),
        P(None, "dp", "tensor"),
        P(None, "dp", "tensor"),
        P("dp", None),
        P("dp"),
    )
    out_specs = (
        P(None, "dp", "tensor"),
        P(None, "dp", "tensor"),
        P(None, "dp", "tensor"),
        P(None, None, "tensor"),
        P("dp", "tensor"),
    )
    return jax.shard_map(body, mesh=mesh, in_specs=in_specs, out_specs=out_specs, check_vma=False)
```

profile of v0, /device:TPU:0, one launch (start us, length us, event | category | flops | bytes accessed | tf_op | source)
XLA Modules:
  0.0 229.7 jit_solution(10080741824321627601)
XLA Ops:
  7.2 0.0 reduce-scatter.2.cloned.1.call-start
  7.2 0.7 reduce-scatter.2.cloned.1.call-update
  7.9 0.0 all-gather.2.cloned.1.call-start
  7.9 71.3 %reduce-scatter.2.cloned.1.call-done = bf16[2,224,2048]{2,1,0:T(8,128)(2,1)} async-done(((bf16[2,896,2048]{2,1,0:T(8,128)(2,1)}), bf16[2,224,2048]{2,1,0:T(8,128)(2,1)}) %reduce-scatter.2.cloned.1.call-update) | async-done | bytes 1835024 | tf_op jit(solution)/shard_map/reduce_scatter | solution.py:15
  79.2 1.7 copy.21
  80.9 47.8 %all_to_all.27 = bf16[2,224,8,256]{3,1,0,2:T(8,128)(2,1)S(1)} all-to-all(bf16[2,224,8,256]{3,1,0,2:T(8,128)(2,1)S(1)} %bitcast.31), channel_id=1, replica_groups=mesh['dp'=4,'tensor'=8] {'tensor'}, dimensions={2} | all-to-all | bytes 3670016 | tf_op jit(solution)/shard_map/all_to_all | solution.py:17
  128.7 0.1 copy.16
  128.8 25.3 %all_to_all.28 = bf16[2,4,2,224,256]{4,3,2,0,1:T(8,128)(2,1)S(1)} all-to-all(bf16[2,4,2,224,256]{4,3,2,0,1:T(8,128)(2,1)S(1)} %copy.16), channel_id=1, replica_groups=mesh['dp'=4,'tensor'=8] {'dp'}, dimensions={1} | all-to-all | bytes 3670016 | tf_op jit(solution)/shard_map/all_to_all | solution.py:21
  154.1 0.4 convert_bitcast_fusion
  154.5 0.0 copy-start.1
  154.5 0.0 copy-start.2
  154.5 0.4 copy.17
  154.9 1.2 copy-done.3
  156.1 1.2 copy-done.1
  157.4 1.0 copy-done.2
  158.4 5.7 %fusion.9 = (bf16[2,1792,256]{2,1,0:T(8,128)(2,1)}, f32[2,1792,256]{2,1,0:T(8,128)}, f32[2,1792,256]{2,1,0:T(8,128)}, f32[2,1792,256]{2,1,0:T(8,128)}) fusion(f32[2,1792,256]{2,1,0:T(8,128)S(1)} %copy-done.1, f32[2,1792,256]{2,1,0:T(8,128)S(1)} %bitcast.29, f32[2,1792,256]{2,1,0:T(8,128)S(1)} %copy-done.2, f32[2,1792,256]{2,1,0:T(8,128)S(1)} %copy-done.3), kind=kLoop, calls=%fused_computation.20 | loop fusion | flops 14680064 | bytes 27525120 | tf_op jit(solution)/shard_map/convert_element_type | solution.py:33
  164.1 0.0 all-gather.2.cloned.1.call-update
  164.1 0.0 copy-done.4
  164.1 5.9 %gather_fusion = bf16[128,7168]{1,0:T(8,128)(2,1)S(1)} fusion(bf16[256,7168]{1,0:T(8,128)(2,1)} %param.10, s32[1024]{0:T(1024)S(1)} %pad_clamp_fusion), kind=kCustom, calls=%fused_computation | custom fusion | bytes 3670528 | tf_op jit(solution)/shard_map/jit(_take)/gather | solution.py:35
  170.0 44.6 %all-gather.2.cloned.1.call-done = bf16[2,7168,256]{2,1,0:T(8,128)(2,1)} async-done(((bf16[2,1792,256]{2,1,0:T(8,128)(2,1)}), bf16[2,7168,256]{2,1,0:T(8,128)(2,1)}) %all-gather.2.cloned.1.call-update) | async-done | bytes 7340048 | tf_op jit(solution)/shard_map/all_gather | solution.py:34
  214.7 4.4 %fusion.1 = f32[128,2,256]{2,0,1:T(8,128)S(1)} fusion(bf16[2,7168,256]{2,1,0:T(8,128)(2,1)} %all-gather.2.cloned.1.call-done, bf16[128,7168]{1,0:T(8,128)(2,1)S(1)} %gather_fusion, pred[128]{0:T(512)(128)(4,1)S(1)} %compare_and_fusion), kind=kOutput, calls=%fused_computation.7 | convolution fusion | flops 940441600 | bytes 9437312 | tf_op jit(solution)/shard_map/rd,kdh->rkh/dot_general | solution.py:36
  219.0 0.7 fusion.7
  219.7 0.1 copy-done
  219.8 3.0 %copy.23 = bf16[2,7168,256]{2,1,0:T(8,128)(2,1)} copy(bf16[2,7168,256]{2,1,0:T(8,128)(2,1)S(1)} %copy-done) | data formatting | bytes 14680064
  (6 shorter events, 0.0 us)
Async XLA Ops:
  7.2 72.0 %reduce-scatter.2.cloned.1.call-start = ((), (), s32[]{:S(2)}) async-start(), calls=%async_computation.3 | async-start | bytes 9175040 | tf_op jit(solution)/shard_map/reduce_scatter | solution.py:15
  7.9 206.7 %all-gather.2.cloned.1.call-start = ((), (), s32[]{:S(2)}) async-start(), calls=%async_computation.4 | async-start | bytes 9175040 | tf_op jit(solution)/shard_map/all_gather | solution.py:34
  154.1 2.0 copy-start.3
  154.5 2.9 %copy-start.1 = (f32[2,1792,256]{2,1,0:T(8,128)S(1)}, f32[2,1792,256]{2,1,0:T(8,128)}, u32[]{:S(2)}) copy-start(f32[2,1792,256]{2,1,0:T(8,128)} %param.7) | copy-start | bytes 11010052
  154.5 3.9 %copy-start.2 = (f32[2,1792,256]{2,1,0:T(8,128)S(1)}, f32[2,1792,256]{2,1,0:T(8,128)}, u32[]{:S(2)}) copy-start(f32[2,1792,256]{2,1,0:T(8,128)} %param.8) | copy-start | bytes 11010052
  158.4 5.7 %copy-start.4 = (s32[128]{0:T(128)S(1)}, s32[128]{0:T(128)}, u32[]{:S(2)}) copy-start(s32[128]{0:T(128)} %param.11) | copy-start | bytes 1540
  214.6 5.2 %copy-start = (bf16[2,7168,256]{2,1,0:T(8,128)(2,1)S(1)}, bf16[2,7168,256]{2,1,0:T(8,128)(2,1)}, u32[]{:S(2)}) copy-start(bf16[2,7168,256]{2,1,0:T(8,128)(2,1)} %all-gather.2.cloned.1.call-done) | copy-start | bytes 22020100
Sparse Core Ops, SparseCore 0:
  10.5 68.6 reduce-scatter.1
  164.2 50.3 all-gather.1
where the time goes:
time: 230 us
  waiting for transfers between devices  117 us (51%)
  blocking collectives  73.1 us (32%)
  local copies, waits for them, and re-layouts  14.7 us (6%)
  between operations  14.1 us (6%)
  other arithmetic  6.75 us (3%)
  matrix products  4.38 us (2%)
    reduce_scatter x1, waiting for transfers between devices, body(): lax.psum_scatter(grad_local, 'dp', scatter_dimension=1, tiled=True)  71.3 us
    all_to_all x1, blocking collectives, body(): lax.all_to_all(pieces.astype(jnp.bfloat16), 'tensor', split_axis=2, conca...  47.8 us
    all_gather x1, waiting for transfers between devices, body(): replicated = lax.all_gather(rollout_shard, 'dp', axis=1, tiled=True)  44.6 us
    all_to_all x1, blocking collectives, body(): lax.all_to_all(spread.astype(jnp.bfloat16), 'dp', split_axis=1, concat_ax...  25.3 us
    unnamed x11, local copies, waits for them, and re-layouts  6.67 us
    gather x1, local copies, waits for them, and re-layouts, body(): picked = jnp.take(tokens, route, axis=0)  5.88 us
    convert_element_type x1, other arithmetic, body(): rollout_shard = new_master.astype(jnp.bfloat16)  5.66 us
  transfers between devices with their start and end apart: 2, of which 2 were waited for; matrix products, arithmetic and copies ran while one was open for 3% of the time, Pallas kernels for 0%

commit v1 on v0

--- a/solution.py
+++ b/solution.py
@@ -1,7 +1,15 @@
+import functools
+
 import jax
 import jax.numpy as jnp
 from jax import lax
+from jax.experimental import pallas as pl
+from jax.experimental.pallas import tpu as pltpu
 from jax.sharding import PartitionSpec as P
+
+MESH = pl.DeviceIdType.MESH
+LANES = 128
+AHEAD = 2
 
 
 def body(grads, master, moment1, moment2, tokens, route):
@@ -38,6 +46,387 @@
     return (new_master, new_moment1, new_moment2, replicated, hidden)
 
 
+def kernel(
+    tensor_count,
+    grads,
+    states,
+    tokens,
+    route,
+    outs,
+    rollout,
+    hidden,
+    mine,
+    theirs,
+    land,
+    crossed,
+    held,
+    roll,
+    token_rows,
+    picked,
+    acc,
+    load_sem,
+    core_send,
+    core_recv,
+    state_sem,
+    token_sem,
+    spread_send,
+    spread_recv,
+    cross_send,
+    cross_recv,
+    near_send,
+    near_recv,
+    far_send,
+    far_recv,
+    relay_send,
+    relay_recv,
+    out_sem,
+    roll_sem,
+):
+    rank = lax.axis_index("dp")
+    place = lax.axis_index("tensor")
+    row, core = rank // 2, rank % 2
+    near = row * 2 + 1 - core
+    far = (1 - row) * 2 + core
+    across = (1 - row) * 2 + 1 - core
+    subs = land.shape[1]
+    slab = mine.shape[0]
+    width = land.shape[4]
+    chunk = picked.shape[2] // tensor_count
+    steps = slab // chunk
+    owner, sub = place // subs, place % subs
+    owner_row, owner_core = owner // 2, owner % 2
+    side = (owner_row + row) % 2
+
+    def rows(step):
+        return pl.ds(pl.multiple_of(step * chunk, chunk), chunk)
+
+    def remote(source, target, send, recv, to_rank, to_place):
+        return pltpu.make_async_remote_copy(
+            src_ref=source,
+            dst_ref=target,
+            send_sem=send,
+            recv_sem=recv,
+            device_id=(to_rank, to_place),
+            device_id_type=MESH,
+        )
+
+    def load(step):
+        return pltpu.make_async_copy(
+            grads.at[0, core, rows(step)], mine.at[rows(step)], load_sem.at[step]
+        )
+
+    def swap(step):
+        return remote(
+            grads.at[0, 1 - core, rows(step)],
+            theirs.at[rows(step)],
+            core_send.at[step],
+            core_recv.at[step],
+            near,
+            place,
+        )
+
+    def state(which, step):
+        return pltpu.make_async_copy(
+            states[which].at[:, :, rows(step)],
+            held.at[which, :, :, rows(step)],
+            state_sem.at[which * steps + step],
+        )
+
+    def state_out(which, step):
+        return pltpu.make_async_copy(
+            held.at[which, :, :, rows(step)],
+            outs[which].at[:, :, rows(step)],
+            out_sem.at[which * steps + step],
+        )
+
+    def landing(step, part, piece, half):
+        return ((step * 2 + part) * subs + piece) * 2 + half
+
+    def spread(step, offset):
+        goal = (place + offset) % tensor_count
+        return remote(
+            mine.at[rows(step), pl.ds(pl.multiple_of(goal * width, width), width)],
+            land.at[side, sub, core, rows(step)],
+            spread_send.at[step * tensor_count + offset],
+            spread_recv.at[landing(step, side, sub, core)],
+            row * 2 + owner_core,
+            goal,
+        )
+
+    def spread_self(step):
+        return pltpu.make_async_copy(
+            mine.at[rows(step), pl.ds(pl.multiple_of(place * width, width), width)],
+            land.at[side, sub, core, rows(step)],
+            spread_recv.at[landing(step, side, sub, core)],
+        )
+
+    def wait_landing(step, part):
+        for piece in range(subs):
+            for half in range(2):
+                spot = land.at[part, piece, half, rows(step)]
+                pltpu.make_async_copy(
+                    spot, spot, spread_recv.at[landing(step, part, piece, half)]
+                ).wait()
+
+    def cross(step):
+        return remote(
+            land.at[1, :, :, rows(step)],
+            crossed.at[:, :, rows(step)],
+            cross_send.at[step],
+            cross_recv.at[step],
+            far,
+            place,
+        )
+
+    def block(of_rank, step):
+        return roll.at[:, pl.ds(of_rank * subs, subs), rows(step)]
+
+    def to_near(of_rank, step):
+        return remote(
+            block(of_rank, step), block(of_rank, step),
+            near_send.at[step], near_recv.at[step], near, place,
+        )
+
+    def to_far(of_rank, step):
+        return remote(
+            block(of_rank, step), block(of_rank, step),
+            far_send.at[step], far_recv.at[step], far, place,
+        )
+
+    def relay(of_rank, step):
+        return remote(
+            block(of_rank, step), block(of_rank, step),
+            relay_send.at[step], relay_recv.at[step], near, place,
+        )
+
+    def roll_out(step):
+        return pltpu.make_async_copy(
+            roll.at[:, :, rows(step)], rollout.at[:, :, rows(step)], roll_sem.at[step]
+        )
+
+    middle = tensor_count // 2
+    order = sorted(range(1, tensor_count), key=lambda i: abs(i - middle))
+
+    def issue(step):
+        load(step).wait()
+        swap(step).wait_recv()
+        strip = 16
+
+        @pl.loop(0, chunk // strip)
+        def _(i):
+            at = pl.ds(pl.multiple_of(step * chunk + i * strip, strip), strip)
+            total = mine[at].astype(jnp.float32) + theirs[at].astype(jnp.float32)
+            mine[at] = total.astype(mine.dtype)
+
+        for offset in order:
+            spread(step, offset).start()
+
+        @pl.when(owner_core == core)
+        def _():
+            spread_self(step).start()
+
+        @pl.when(owner_core != core)
+        def _():
+            spread(step, 0).start()
+
+    def issued(step):
+        for offset in order:
+            spread(step, offset).wait_send()
+
+        @pl.when(owner_core != core)
+        def _():
+            spread(step, 0).wait_send()
+
+    first_fix = 1.0 - 0.9**10
+    second_fix = 1.0 - 0.95**10
+
+    def update(step):
+        wait_landing(step, 0)
+        cross(step).wait_recv()
+        for which in range(3):
+            state(which, step).wait()
+        strip = 16
+        tiles = chunk // strip
+
+        @pl.loop(0, tiles)
+        def _(i):
+            at = pl.ds(pl.multiple_of(step * chunk + i * strip, strip), strip)
+            for half in range(2):
+                for piece in range(subs):
+                    grad = land[0, piece, half, at].astype(jnp.float32)
+                    grad = grad + crossed[piece, half, at].astype(jnp.float32)
+                    old = held[0, half, piece, at]
+                    moment1 = 0.9 * held[1, half, piece, at] + 0.1 * grad
+                    moment2 = 0.95 * held[2, half, piece, at] + 0.05 * grad * grad
+                    scaled = jnp.sqrt(moment2 * (1.0 / second_fix)) + 1e-08
+                    change = moment1 * (1.0 / first_fix) / scaled + 0.1 * old
+                    new = old - 0.003 * change
+                    held[0, half, piece, at] = new
+                    held[1, half, piece, at] = moment1
+                    held[2, half, piece, at] = moment2
+                    roll[half, rank * subs + piece, at] = new.astype(roll.dtype)
+
+        to_far(rank, step).start()
+        to_near(rank, step).start()
+        for which in range(3):
+            state_out(which, step).start()
+
+    def pass_on(step):
+        to_far(far, step).wait_recv()
+        relay(far, step).start()
+
+    def multiply(step):
+        to_near(near, step).wait_recv()
+        relay(across, step).wait_recv()
+        roll_out(step).start()
+        for half in range(2):
+            weights = roll[half, :, rows(step)].reshape(tensor_count * chunk, width)
+            acc[half] += jnp.dot(
+                picked[step], weights, preferred_element_type=jnp.float32
+            )
+
+    @pl.loop(0, steps)
+    def _(step):
+        swap(step).start()
+        load(step).start()
+
+    token_copy = pltpu.make_async_copy(tokens, token_rows, token_sem)
+    for ahead in range(AHEAD):
+        issue(ahead)
+    token_copy.start()
+
+    @pl.loop(0, steps)
+    def _(step):
+        for which in range(3):
+            state(which, step).start()
+
+    acc[...] = jnp.zeros_like(acc)
+    token_copy.wait()
+    lanes = lax.broadcasted_iota(jnp.int32, (route.shape[0], token_rows.shape[0]), 1)
+    chosen = jnp.where(lanes == route[...], 1.0, 0.0).astype(token_rows.dtype)
+
+    @pl.loop(0, tensor_count)
+    def _(part):
+        for step in range(steps):
+            at = pl.ds(pl.multiple_of(part * slab + step * chunk, chunk), chunk)
+            some = jnp.dot(chosen, token_rows[:, at], preferred_element_type=jnp.float32)
+            to = pl.ds(pl.multiple_of(part * chunk, chunk), chunk)
+            picked[step, :, to] = some.astype(picked.dtype)
+
+    @pl.loop(0, steps + 3)
+    def _(now):
+        @pl.when((now >= 1) & (now < steps + 1))
+        def _():
+            update(now - 1)
+
+        @pl.when(now < steps)
+        def _():
+            wait_landing(now, 1)
+            cross(now).start()
+            issued(now)
+
+        @pl.when(now < steps - AHEAD)
+        def _():
+            issue(now + AHEAD)
+
+        @pl.when((now >= 2) & (now < steps + 2))
+        def _():
+            pass_on(now - 2)
+
+        @pl.when(now >= 3)
+        def _():
+            multiply(now - 3)
+
+    gate, up = acc[0], acc[1]
+    hidden[...] = (gate / (1.0 + jnp.exp(-gate)) * up).astype(hidden.dtype)
+
+    @pl.loop(0, steps)
+    def _(step):
+        swap(step).wait_send()
+        cross(step).wait_send()
+        to_far(rank, step).wait_send()
+        to_near(rank, step).wait_send()
+        relay(far, step).wait_send()
+        roll_out(step).wait()
+        for which in range(3):
+            state_out(which, step).wait()
+
+
+def entry(tensor_count, grads, s0, s1, s2, tokens, route, o0, o1, o2, *rest):
+    kernel(tensor_count, grads, (s0, s1, s2), tokens, route, (o0, o1, o2), *rest)
+
+
+def fused(grads, master, moment1, moment2, tokens, route):
+    tensor_count = lax.axis_size("tensor")
+    rank_count = lax.axis_size("dp")
+    subs = tensor_count // rank_count
+    slab, hidden_width = grads.shape[2:]
+    width = hidden_width // tensor_count
+    steps = slab // LANES
+    routed = route.shape[0]
+    split = (2, subs, slab, width)
+    states = [array.reshape(split) for array in (master, moment1, moment2)]
+    anywhere = pl.BlockSpec(memory_space=pl.ANY)
+    vmem = pl.BlockSpec(memory_space=pltpu.VMEM)
+    dma = pltpu.SemaphoreType.DMA
+    half = jnp.bfloat16
+    f32 = jnp.float32
+    new_master, new1, new2, rollout, hidden = pl.pallas_call(
+        functools.partial(entry, tensor_count),
+        out_shape=[jax.ShapeDtypeStruct(split, f32)] * 3
+        + [
+            jax.ShapeDtypeStruct((2, tensor_count, slab, width), half),
+            jax.ShapeDtypeStruct((routed, width), half),
+        ],
+        in_specs=[anywhere] * 5 + [vmem],
+        out_specs=[anywhere] * 4 + [vmem],
+        scratch_shapes=[
+            pltpu.VMEM((slab, hidden_width), half),
+            pltpu.VMEM((slab, hidden_width), half),
+            pltpu.VMEM((2, subs, 2, slab, width), half),
+            pltpu.VMEM((subs, 2, slab, width), half),
+            pltpu.VMEM((3,) + split, f32),
+            pltpu.VMEM((2, tensor_count, slab, width), half),
+            pltpu.VMEM(tokens.shape, half),
+            pltpu.VMEM((steps, routed, tensor_count * LANES), half),
+            pltpu.VMEM((2, routed, width), f32),
+            dma((steps,)),
+            dma((steps,)),
+            dma((steps,)),
+            dma((3 * steps,)),
+            dma,
+            dma((steps * tensor_count,)),
+            dma((steps * 2 * subs * 2,)),
+        ]
+        + [dma((steps,))] * 8
+        + [dma((3 * steps,)), dma((steps,))],
+        compiler_params=pltpu.CompilerParams(
+            has_side_effects=True, vmem_limit_bytes=56 * 1024 * 1024
+        ),
+    )(grads, *states, tokens, route.reshape(routed, 1))
+    whole = (2, subs * slab, width)
+    return (
+        new_master.reshape(whole),
+        new1.reshape(whole),
+        new2.reshape(whole),
+        rollout.reshape(2, tensor_count * slab, width),
+        hidden,
+    )
+
+
+def chosen_body(grads, *rest):
+    tensor_count, rank_count = lax.axis_size("tensor"), lax.axis_size("dp")
+    slab, hidden_width = grads.shape[2:]
+    fits = (
+        rank_count == 4
+        and tensor_count % rank_count == 0
+        and slab % LANES == 0
+        and slab // LANES > AHEAD
+        and hidden_width % (tensor_count * LANES) == 0
+    )
+    return fused(grads, *rest) if fits else body(grads, *rest)
+
+
 def solution(mesh):
     in_specs = (
         P("dp", None, "tensor", None),
@@ -54,4 +443,4 @@
         P(None, None, "tensor"),
         P("dp", "tensor"),
     )
-    return jax.shard_map(body, mesh=mesh, in_specs=in_specs, out_specs=out_specs, check_vma=False)
+    return jax.shard_map(chosen_body, mesh=mesh, in_specs=in_specs, out_specs=out_specs, check_vma=False)

time: 230 us -> 144 us (0.63)
  the two profiles are of different devices: /device:TPU:0 before, /device:TPU:11 now
where the time goes in v1:
time: 144 us
  Pallas kernels  128 us (89%)
  local copies, waits for them, and re-layouts  15.5 us (11%)
    pallas_call x1, Pallas kernels, fused(): pl.pallas_call(functools.partial(entry, tensor_count), out_shape=[jax.Sha...  128 us
    unnamed x13, local copies, waits for them, and re-layouts  14.1 us

profile of v1, /device:TPU:11, one launch (start us, length us, event | category | flops | bytes accessed | tf_op | source)
XLA Modules:
  0.0 143.8 jit_solution(13282450769441947511)
XLA Ops:
  0.6 1.4 copy.11.route
  2.0 127.7 %shard_map.101 = (f32[2,2,896,256]{3,2,1,0:T(8,128)}, f32[2,2,896,256]{3,2,1,0:T(8,128)}, f32[2,2,896,256]{3,2,1,0:T(8,128)}, bf16[2,8,896,256]{3,2,1,0:T(8,128)(2,1)}, bf16[128,256]{1,0:T(8,128)(2,1)}) custom-call(bf16[1,2,896,2048]{3,2,1,0:T(8,128)(2,1)} %grads.1, f32[2,2,896,256]{3,2,1,0:T(8,128)} %bitcast.14, f32[2,2,896,256]{3,2,1,0:T(8,128)} %bitcast.15, ...), custom_call_target="tpu_custom_call" | custom-call | tf_op jit(solution)/shard_map/pallas_call | solution.py:374
  129.7 0.0 slice-start
  129.7 4.3 %copy.17 = f32[2,1792,256]{2,1,0:T(8,128)} copy(f32[2,1792,256]{2,1,0:T(8,128)} %bitcast.13) | data formatting | bytes 7340032
  134.0 0.0 copy-start
  134.0 0.0 slice-start.1
  134.0 4.3 %copy.18 = f32[2,1792,256]{2,1,0:T(8,128)} copy(f32[2,1792,256]{2,1,0:T(8,128)} %bitcast.12) | data formatting | bytes 7340032
  138.3 0.0 copy-done
  138.3 1.8 %copy.19 = f32[2,1792,256]{2,1,0:T(8,128)} copy(f32[2,1792,256]{2,1,0:T(8,128)S(1)} %bitcast.11) | data formatting | bytes 7340032
  140.1 0.0 slice-done
  140.1 0.0 slice-done.1
  140.1 0.0 copy-start.1
  140.1 3.1 %copy.20 = bf16[2,7168,256]{2,1,0:T(8,128)(2,1)} copy(bf16[2,7168,256]{2,1,0:T(8,128)(2,1)S(1)} %bitcast.10) | data formatting | bytes 14680064
  143.2 0.0 copy-done.1
  143.2 0.6 copy.21
  (1 shorter events, 0.0 us)
Async XLA Ops:
  129.7 10.4 %slice-start = ((s8[7340032]{0:T(1024)(128)(4,1)}), s8[4194304]{0:T(1024)(128)(4,1)S(1)}, s32[]{:S(2)}) async-start(s8[7340032]{0:T(1024)(128)(4,1)} %bitcast.8), calls=%async_computation | async-start | bytes 8388608
  134.0 4.3 %copy-start = (f32[2,2,896,256]{3,2,1,0:T(8,128)S(1)}, f32[2,2,896,256]{3,2,1,0:T(8,128)}, u32[]{:S(2)}) copy-start(f32[2,2,896,256]{3,2,1,0:T(8,128)} %get-tuple-element.12) | copy-start | bytes 11010052
  134.0 6.2 %slice-start.1 = ((s8[7340032]{0:T(1024)(128)(4,1)}), s8[3145728]{0:T(1024)(128)(4,1)S(1)}, s32[]{:S(2)}) async-start(s8[7340032]{0:T(1024)(128)(4,1)} %bitcast.8), calls=%async_computation.1 | async-start | bytes 6291456
  140.1 3.1 %copy-start.1 = (bf16[128,256]{1,0:T(8,128)(2,1)S(1)}, bf16[128,256]{1,0:T(8,128)(2,1)}, u32[]{:S(2)}) copy-start(bf16[128,256]{1,0:T(8,128)(2,1)} %get-tuple-element.24) | copy-start | bytes 196612

commit v2 on v1

--- a/solution.py
+++ b/solution.py
@@ -9,7 +9,8 @@
 
 MESH = pl.DeviceIdType.MESH
 LANES = 128
-AHEAD = 2
+CHUNK = 64
+AHEAD = 4
 
 
 def body(grads, master, moment1, moment2, tokens, route):
@@ -52,17 +53,16 @@
     states,
     tokens,
     route,
-    outs,
-    rollout,
+    held,
+    roll,
     hidden,
     mine,
     theirs,
     land,
     crossed,
-    held,
-    roll,
     token_rows,
     picked,
+    chosen,
     acc,
     load_sem,
     core_send,
@@ -79,8 +79,6 @@
     far_recv,
     relay_send,
     relay_recv,
-    out_sem,
-    roll_sem,
 ):
     rank = lax.axis_index("dp")
     place = lax.axis_index("tensor")
@@ -91,8 +89,9 @@
     subs = land.shape[1]
     slab = mine.shape[0]
     width = land.shape[4]
-    chunk = picked.shape[2] // tensor_count
+    chunk = CHUNK
     steps = slab // chunk
+    pairs = slab // LANES
     owner, sub = place // subs, place % subs
     owner_row, owner_core = owner // 2, owner % 2
     side = (owner_row + row) % 2
@@ -128,15 +127,8 @@
     def state(which, step):
         return pltpu.make_async_copy(
             states[which].at[:, :, rows(step)],
-            held.at[which, :, :, rows(step)],
+            held[which].at[:, :, rows(step)],
             state_sem.at[which * steps + step],
-        )
-
-    def state_out(which, step):
-        return pltpu.make_async_copy(
-            held.at[which, :, :, rows(step)],
-            outs[which].at[:, :, rows(step)],
-            out_sem.at[which * steps + step],
         )
 
     def landing(step, part, piece, half):
@@ -199,13 +191,8 @@
             relay_send.at[step], relay_recv.at[step], near, place,
         )
 
-    def roll_out(step):
-        return pltpu.make_async_copy(
-            roll.at[:, :, rows(step)], rollout.at[:, :, rows(step)], roll_sem.at[step]
-        )
-
     middle = tensor_count // 2
-    order = sorted(range(1, tensor_count), key=lambda i: abs(i - middle))
+    order = sorted(range(1, tensor_count), key=lambda i: -abs(i - middle))
 
     def issue(step):
         load(step).wait()
@@ -255,35 +242,43 @@
                 for piece in range(subs):
                     grad = land[0, piece, half, at].astype(jnp.float32)
                     grad = grad + crossed[piece, half, at].astype(jnp.float32)
-                    old = held[0, half, piece, at]
-                    moment1 = 0.9 * held[1, half, piece, at] + 0.1 * grad
-                    moment2 = 0.95 * held[2, half, piece, at] + 0.05 * grad * grad
+                    old = held[0][half, piece, at]
+                    moment1 = 0.9 * held[1][half, piece, at] + 0.1 * grad
+                    moment2 = 0.95 * held[2][half, piece, at] + 0.05 * grad * grad
                     scaled = jnp.sqrt(moment2 * (1.0 / second_fix)) + 1e-08
                     change = moment1 * (1.0 / first_fix) / scaled + 0.1 * old
                     new = old - 0.003 * change
-                    held[0, half, piece, at] = new
-                    held[1, half, piece, at] = moment1
-                    held[2, half, piece, at] = moment2
+                    held[0][half, piece, at] = new
+                    held[1][half, piece, at] = moment1
+                    held[2][half, piece, at] = moment2
                     roll[half, rank * subs + piece, at] = new.astype(roll.dtype)
 
         to_far(rank, step).start()
         to_near(rank, step).start()
-        for which in range(3):
-            state_out(which, step).start()
 
     def pass_on(step):
         to_far(far, step).wait_recv()
         relay(far, step).start()
 
-    def multiply(step):
-        to_near(near, step).wait_recv()
-        relay(across, step).wait_recv()
-        roll_out(step).start()
+    def multiply(pair):
+        for part in range(LANES // chunk):
+            step = pair * (LANES // chunk) + part
+            to_near(near, step).wait_recv()
+            relay(across, step).wait_recv()
+        at = pl.ds(pl.multiple_of(pair * LANES, LANES), LANES)
         for half in range(2):
-            weights = roll[half, :, rows(step)].reshape(tensor_count * chunk, width)
+            weights = roll[half, :, at].reshape(tensor_count * LANES, width)
             acc[half] += jnp.dot(
-                picked[step], weights, preferred_element_type=jnp.float32
+                picked[pair], weights, preferred_element_type=jnp.float32
             )
+
+    def pick(pair):
+        for part in range(tensor_count):
+            at = pl.ds(pl.multiple_of(part * slab + pair * LANES, LANES), LANES)
+            some = jnp.dot(
+                chosen[...], token_rows[:, at], preferred_element_type=jnp.float32
+            )
+            picked[pair, :, part * LANES : (part + 1) * LANES] = some.astype(picked.dtype)
 
     @pl.loop(0, steps)
     def _(step):
@@ -301,24 +296,13 @@
             state(which, step).start()
 
     acc[...] = jnp.zeros_like(acc)
-    token_copy.wait()
-    lanes = lax.broadcasted_iota(jnp.int32, (route.shape[0], token_rows.shape[0]), 1)
-    chosen = jnp.where(lanes == route[...], 1.0, 0.0).astype(token_rows.dtype)
-
-    @pl.loop(0, tensor_count)
-    def _(part):
-        for step in range(steps):
-            at = pl.ds(pl.multiple_of(part * slab + step * chunk, chunk), chunk)
-            some = jnp.dot(chosen, token_rows[:, at], preferred_element_type=jnp.float32)
-            to = pl.ds(pl.multiple_of(part * chunk, chunk), chunk)
-            picked[step, :, to] = some.astype(picked.dtype)
-
-    @pl.loop(0, steps + 3)
+    index = lax.broadcasted_iota(jnp.int32, (token_rows.shape[0], route.shape[1]), 0)
+    onehot = jnp.where(index == route[...], 1.0, 0.0)
+    chosen[...] = onehot.T.astype(chosen.dtype)
+    per = LANES // chunk
+
+    @pl.loop(0, steps + 4)
     def _(now):
-        @pl.when((now >= 1) & (now < steps + 1))
-        def _():
-            update(now - 1)
-
         @pl.when(now < steps)
         def _():
             wait_landing(now, 1)
@@ -329,13 +313,25 @@
         def _():
             issue(now + AHEAD)
 
-        @pl.when((now >= 2) & (now < steps + 2))
-        def _():
-            pass_on(now - 2)
-
-        @pl.when(now >= 3)
-        def _():
-            multiply(now - 3)
+        @pl.when(now == 0)
+        def _():
+            token_copy.wait()
+
+        @pl.when(now < pairs)
+        def _():
+            pick(now)
+
+        @pl.when((now >= 1) & (now < steps + 1))
+        def _():
+            update(now - 1)
+
+        @pl.when((now >= 3) & (now < steps + 3))
+        def _():
+            pass_on(now - 3)
+
+        @pl.when((now >= 4) & ((now - 4) % per == per - 1))
+        def _():
+            multiply((now - 4) // per)
 
     gate, up = acc[0], acc[1]
     hidden[...] = (gate / (1.0 + jnp.exp(-gate)) * up).astype(hidden.dtype)
@@ -347,9 +343,6 @@
         to_far(rank, step).wait_send()
         to_near(rank, step).wait_send()
         relay(far, step).wait_send()
-        roll_out(step).wait()
-        for which in range(3):
-            state_out(which, step).wait()
 
 
 def entry(tensor_count, grads, s0, s1, s2, tokens, route, o0, o1, o2, *rest):
@@ -362,7 +355,7 @@
     subs = tensor_count // rank_count
     slab, hidden_width = grads.shape[2:]
     width = hidden_width // tensor_count
-    steps = slab // LANES
+    steps = slab // CHUNK
     routed = route.shape[0]
     split = (2, subs, slab, width)
     states = [array.reshape(split) for array in (master, moment1, moment2)]
@@ -373,22 +366,21 @@
     f32 = jnp.float32
     new_master, new1, new2, rollout, hidden = pl.pallas_call(
         functools.partial(entry, tensor_count),
-        out_shape=[jax.ShapeDtypeStruct(split, f32)] * 3
+        out_shape=[pltpu.VMEM(split, f32)] * 3
         + [
-            jax.ShapeDtypeStruct((2, tensor_count, slab, width), half),
-            jax.ShapeDtypeStruct((routed, width), half),
+            pltpu.VMEM((2, tensor_count, slab, width), half),
+            pltpu.VMEM((routed, width), half),
         ],
         in_specs=[anywhere] * 5 + [vmem],
-        out_specs=[anywhere] * 4 + [vmem],
+        out_specs=[vmem] * 5,
         scratch_shapes=[
             pltpu.VMEM((slab, hidden_width), half),
             pltpu.VMEM((slab, hidden_width), half),
             pltpu.VMEM((2, subs, 2, slab, width), half),
             pltpu.VMEM((subs, 2, slab, width), half),
-            pltpu.VMEM((3,) + split, f32),
-            pltpu.VMEM((2, tensor_count, slab, width), half),
             pltpu.VMEM(tokens.shape, half),
-            pltpu.VMEM((steps, routed, tensor_count * LANES), half),
+            pltpu.VMEM((slab // LANES, routed, tensor_count * LANES), half),
+            pltpu.VMEM((routed, tokens.shape[0]), half),
             pltpu.VMEM((2, routed, width), f32),
             dma((steps,)),
             dma((steps,)),
@@ -398,12 +390,11 @@
             dma((steps * tensor_count,)),
             dma((steps * 2 * subs * 2,)),
         ]
-        + [dma((steps,))] * 8
-        + [dma((3 * steps,)), dma((steps,))],
+        + [dma((steps,))] * 8,
         compiler_params=pltpu.CompilerParams(
-            has_side_effects=True, vmem_limit_bytes=56 * 1024 * 1024
+            has_side_effects=True, vmem_limit_bytes=45 * 1024 * 1024
         ),
-    )(grads, *states, tokens, route.reshape(routed, 1))
+    )(grads, *states, tokens, route.reshape(1, routed))
     whole = (2, subs * slab, width)
     return (
         new_master.reshape(whole),
@@ -421,7 +412,7 @@
         rank_count == 4
         and tensor_count % rank_count == 0
         and slab % LANES == 0
-        and slab // LANES > AHEAD
+        and slab // CHUNK > AHEAD
         and hidden_width % (tensor_count * LANES) == 0
     )
     return fused(grads, *rest) if fits else body(grads, *rest)

time: 144 us -> 127 us (0.88)
  the two profiles are of different devices: /device:TPU:11 before, /device:TPU:0 now
where the time goes in v2:
time: 127 us; the launch traced here: 126 us
  Pallas kernels  116 us (91%)
  local copies, waits for them, and re-layouts  9.19 us (7%)
    pallas_call x1, Pallas kernels, fused(): pl.pallas_call(functools.partial(entry, tensor_count), out_shape=[pltpu.V...  116 us
    unnamed x5, local copies, waits for them, and re-layouts  9.19 us

profile of v2, /device:TPU:0, one launch (start us, length us, event | category | flops | bytes accessed | tf_op | source)
XLA Modules:
  0.0 126.3 jit_solution(8802853111442607987)
XLA Ops:
  0.6 116.4 %shard_map.101 = (f32[2,2,896,256]{3,2,1,0:T(8,128)S(1)}, f32[2,2,896,256]{3,2,1,0:T(8,128)S(1)}, f32[2,2,896,256]{3,2,1,0:T(8,128)S(1)}, bf16[2,8,896,256]{3,2,1,0:T(8,128)(2,1)S(1)}, bf16[128,256]{1,0:T(8,128)(2,1)S(1)}) custom-call(bf16[1,2,896,2048]{3,2,1,0:T(8,128)(2,1)} %grads.1, f32[2,2,896,256]{3,2,1,0:T(8,128)} %bitcast.12, ...), custom_call_target="tpu_custom_call" | custom-call | tf_op jit(solution)/shard_map/pallas_call | solution.py:367
  117.1 1.8 %copy.16 = f32[2,1792,256]{2,1,0:T(8,128)} copy(f32[2,1792,256]{2,1,0:T(8,128)S(1)} %bitcast.11) | data formatting | bytes 7340032
  118.9 1.8 %copy.17 = f32[2,1792,256]{2,1,0:T(8,128)} copy(f32[2,1792,256]{2,1,0:T(8,128)S(1)} %bitcast.10) | data formatting | bytes 7340032
  120.8 0.6 copy.20
  121.4 1.8 %copy.18 = f32[2,1792,256]{2,1,0:T(8,128)} copy(f32[2,1792,256]{2,1,0:T(8,128)S(1)} %bitcast.9) | data formatting | bytes 7340032
  123.2 3.0 %copy.19 = bf16[2,7168,256]{2,1,0:T(8,128)(2,1)} copy(bf16[2,7168,256]{2,1,0:T(8,128)(2,1)S(1)} %bitcast.8) | data formatting | bytes 14680064
